TPU v7x, 32 devices: a whole 2x2x4 slice. The times are simulated.
32 devices in a mesh: row: 8 (over z, core), col: 4 (over y, x).
Axes of the slice: x: 2, y: 2, z: 4, core: 2. Of those that a mesh axis runs over, the one named last changes fastest.
Arguments:
- inverse_tiles: bfloat16 [12288, 12288], P('row', 'col'), may hold values from -6 to 6
- factor: bfloat16 [12288, 2048], P('row', 'col'), may hold values from -0.0546875 to 0.0546875
- block_mask: int32 [96, 16], replicated, may hold values 0 or 1
- diag_inverse: float32 [16, 128, 128], replicated, may hold values from -6 to 6
Outputs:
- off_block: bfloat16 [2048, 12288], P('col', 'row')
- diag_block: float32 [16, 128, 128], P('col')
All inputs are finite; a program needn't handle non-finite values.
Results may differ from a plain program's by a relative error of at most 0.012.
Values may be sent and summed in bfloat16 or wider, within the bound.
No kernel may reach another device: no remote copies, remote signals or barrier semaphores. Data moves between devices by JAX's collectives and lax.ppermute only.
A program may use at most 128 MiB of HBM per device.

v0:
```python
import jax
import jax.numpy as jnp
from jax import lax
from jax.sharding import PartitionSpec as P


def from_root(value, axis, source):
    kept = jnp.where(lax.axis_index(axis) == source, value, 0).astype(value.dtype)
    return lax.psum(kept, axis)


def per_device(inverse_tiles, factor, block_mask, diag_inverse):
    rows_here, cols_here = factor.shape
    block_width = diag_inverse.shape[1]
    sup_here = cols_here // block_width
    blocks_here = rows_here // block_width
    row_index = lax.axis_index("row")
    col_index = lax.axis_index("col")
    mask_here = lax.dynamic_slice(
        block_mask, (row_index * blocks_here, col_index * sup_here), (blocks_here, sup_here)
    )
    keep_mask = jnp.repeat(jnp.repeat(mask_here, block_width, 0), block_width, 1).astype(
        jnp.bfloat16
    )
    masked = factor * keep_mask
    full_rows = lax.all_gather(masked, "col", axis=1, tiled=True)
    row_ratio = lax.axis_size("row") // lax.axis_size("col")
    row_pieces = []
    for offset in range(row_ratio):
        row_pieces.append(from_root(full_rows, "row", row_ratio * col_index + offset))
    summed = jnp.zeros((full_rows.shape[1], rows_here), jnp.float32)
    for offset in range(row_ratio):
        columns = row_pieces[offset]
        inverse_part = inverse_tiles[:, offset * rows_here : (offset + 1) * rows_here]
        summed = summed + lax.dot_general(
            columns, inverse_part, (((0,), (1,)), ((), ())), preferred_element_type=jnp.float32
        )
    reduced = lax.psum_scatter(summed, "col", scatter_dimension=0, tiled=True)
    left_factor = masked.astype(jnp.float32).reshape(rows_here, sup_here, block_width)
    right_product = reduced.reshape(sup_here, block_width, rows_here)
    partial_diag = jnp.einsum(
        "jbr,rja->jab", right_product, left_factor, precision=lax.Precision.HIGHEST
    )
    summed_diag = lax.psum(partial_diag.astype(jnp.bfloat16), "row").astype(jnp.float32)
    own_diag = lax.dynamic_slice_in_dim(diag_inverse, col_index * sup_here, sup_here, 0)
    return ((-reduced).astype(jnp.bfloat16), own_diag + summed_diag)


def solution(mesh):
    return jax.shard_map(
        per_device,
        mesh=mesh,
        in_specs=(P("row", "col"), P("row", "col"), P(), P()),
        out_specs=(P("col", "row"), P("col", None, None)),
        check_vma=False,
    )
```

profile of v0, /device:TPU:0, one launch (start us, length us, event | category | flops | bytes accessed | tf_op | source)
XLA Modules:
  0.0 571.0 jit_solution(12963636259537801392)
XLA Ops:
  7.2 0.0 all-gather.2.cloned.1.call-start
  7.2 0.8 dynamic-slice_convert_fusion
  8.0 0.1 copy.6
  8.1 0.1 broadcast_in_dim.11
  8.2 1.9 broadcast_in_dim.12
  10.1 2.8 bitcast_multiply_fusion
  12.9 0.0 all-gather.2.cloned.1.call-update
  12.9 0.0 all-reduce.6.cloned.1.call-start
  12.9 72.7 %all-gather.2.cloned.1.call-done = bf16[1536,2048]{1,0:T(8,128)(2,1)} async-done(((bf16[1536,512]{1,0:T(8,128)(2,1)}), bf16[1536,2048]{1,0:T(8,128)(2,1)}) %all-gather.2.cloned.1.call-update) | async-done | bytes 6291472 | tf_op jit(solution)/shard_map/all_gather | solution.py:26
  85.7 8.1 %broadcast_select_fusion = (bf16[1536,2048]{1,0:T(8,128)(2,1)}, bf16[1536,2048]{1,0:T(8,128)(2,1)}) fusion(bf16[1536,2048]{1,0:T(8,128)(2,1)} %all-gather.2.cloned.1.call-done, pred[]{:T(512)S(6)} %eq.7, pred[]{:T(512)S(6)} %eq.6), kind=kLoop, calls=%fused_computation.1 | loop fusion | flops 6291456 | bytes 18874370 | tf_op jit(solution)/shard_map/jit(_where)/select_n | solution.py:8
  93.8 0.0 slice-start
  93.8 0.0 all-reduce.6.cloned.1.call-update
  93.8 0.0 reduce-scatter.2.cloned.1.call-start
  93.9 254.7 %all-reduce.6.cloned.1.call-done = (bf16[1536,2048]{1,0:T(8,128)(2,1)}, bf16[1536,2048]{1,0:T(8,128)(2,1)}) async-done(((bf16[1536,2048]{1,0:T(8,128)(2,1)}, bf16[1536,2048]{1,0:T(8,128)(2,1)}), (bf16[1536,2048]{1,0:T(8,128)(2,1)}, bf16[1536,2048]{1,0:T(8,128)(2,1)})) %all-reduce.6.cloned.1.call-update) | async-done | bytes 12582928 | tf_op jit(solution)/shard_map/psum | solution.py:9
  348.6 0.0 slice-start.1
  348.6 0.0 slice-start.2
  348.6 16.3 %fusion.1 = f32[2048,1536]{1,0:T(8,128)} fusion(bf16[1536,2048]{1,0:T(8,128)(2,1)} %get-tuple-element.2, bf16[1536,3072]{1,0:T(8,128)(2,1)} %param.4), kind=kOutput, calls=%fused_computation.4 | convolution fusion | flops 9663676416 | bytes 23592960 | tf_op jit(solution)/shard_map/dot_general | solution.py:35
  364.8 0.0 slice-done
  364.9 0.0 slice-done.1
  364.9 0.0 slice-done.2
  364.9 16.9 %convolution_add_fusion = f32[2048,1536]{1,0:T(8,128)} fusion(f32[2048,1536]{1,0:T(8,128)} %fusion.1, bf16[1536,2048]{1,0:T(8,128)(2,1)} %get-tuple-element.3, bf16[1536,3072]{1,0:T(8,128)(2,1)S(1)} %bitcast.15), kind=kOutput, calls=%fused_computation | convolution fusion | flops 9666822144 | bytes 36175872 | tf_op jit(solution)/shard_map/dot_general | solution.py:35
  381.8 0.0 reduce-scatter.2.cloned.1.call-update
  381.8 0.2 all-reduce.4.cloned.1.call-start
  382.1 1.2 copy-done
  383.2 1.6 copy.8
  384.8 118.0 %reduce-scatter.2.cloned.1.call-done = f32[512,1536]{1,0:T(8,128)} async-done(((f32[2048,1536]{1,0:T(8,128)}), f32[512,1536]{1,0:T(8,128)}) %reduce-scatter.2.cloned.1.call-update) | async-done | bytes 3145744 | tf_op jit(solution)/shard_map/reduce_scatter | solution.py:38
  502.7 4.8 convolution_convert_fusion
  507.6 0.0 all-reduce.4.cloned.1.call-update
  507.6 0.0 copy-done.1
  507.6 1.5 negate_convert_fusion
  509.1 53.6 %all-reduce.4.cloned.1.call-done = bf16[4,128,128]{2,1,0:T(8,128)(2,1)} async-done(((bf16[4,128,128]{2,1,0:T(8,128)(2,1)}), bf16[4,128,128]{2,1,0:T(8,128)(2,1)}) %all-reduce.4.cloned.1.call-update) | async-done | bytes 131088 | tf_op jit(solution)/shard_map/psum | solution.py:44
  562.7 1.7 convert_add_fusion
  (3 shorter events, 0.0 us)
Async XLA Ops:
  7.2 78.5 %all-gather.2.cloned.1.call-start = ((), (), s32[]{:S(2)}) async-start(), calls=%async_computation.1 | async-start | bytes 7864320 | tf_op jit(solution)/shard_map/all_gather | solution.py:26
  12.9 335.7 %all-reduce.6.cloned.1.call-start = ((), (), s32[]{:S(2)}) async-start(), calls=%async_computation.4 | async-start | bytes 25165824 | tf_op jit(solution)/shard_map/psum | solution.py:9
  93.8 271.1 %slice-start = ((s8[9437184]{0:T(1024)(128)(4,1)}), s8[1048576]{0:T(1024)(128)(4,1)S(1)}, s32[]{:S(2)}) async-start(s8[9437184]{0:T(1024)(128)(4,1)} %bitcast.14), calls=%async_computation.5 | async-start | bytes 2097152
  93.8 408.9 %reduce-scatter.2.cloned.1.call-start = ((), (), s32[]{:S(2)}) async-start(), calls=%async_computation.2 | async-start | bytes 15728640 | tf_op jit(solution)/shard_map/reduce_scatter | solution.py:38
  348.6 16.3 %slice-start.1 = ((s8[9437184]{0:T(1024)(128)(4,1)}), s8[4194304]{0:T(1024)(128)(4,1)S(1)}, s32[]{:S(2)}) async-start(s8[9437184]{0:T(1024)(128)(4,1)} %bitcast.14), calls=%async_computation.6 | async-start | bytes 8388608
  348.6 16.3 %slice-start.2 = ((s8[9437184]{0:T(1024)(128)(4,1)}), s8[4194304]{0:T(1024)(128)(4,1)S(1)}, s32[]{:S(2)}) async-start(s8[9437184]{0:T(1024)(128)(4,1)} %bitcast.14), calls=%async_computation.7 | async-start | bytes 8388608
  381.8 1.4 copy-start
  381.8 180.9 %all-reduce.4.cloned.1.call-start = ((), (), s32[]{:S(2)}) async-start(), calls=%async_computation.3 | async-start | bytes 262144 | tf_op jit(solution)/shard_map/psum | solution.py:44
  502.7 4.9 copy-start.1
Sparse Core Ops, SparseCore 0:
  13.0 72.6 all-gather.1
  93.9 254.5 all-reduce.5
  381.9 120.7 reduce-scatter.1
  507.7 54.9 all-reduce.3
where the time goes:
time: 571 us
  waiting for transfers between devices  499 us (87%)
  matrix products  38 us (7%)
  other arithmetic  14.9 us (3%)
  between operations  13.8 us (2%)
    psum x1, waiting for transfers between devices, from_root(): return lax.psum(kept, axis)  255 us
    reduce_scatter x1, waiting for transfers between devices, per_device(): reduced = lax.psum_scatter(summed, 'col', scatter_dimension=0, tiled=True)  118 us
    all_gather x1, waiting for transfers between devices, per_device(): full_rows = lax.all_gather(masked, 'col', axis=1, tiled=True)  72.7 us
    psum x1, waiting for transfers between devices, per_device(): lax.psum(partial_diag.astype(jnp.bfloat16), 'row').astype(jnp.float32)  53.6 us
    dot_general x2, matrix products, per_device(): lax.dot_general(columns, inverse_part, (((0,), (1,)), ((), ())), preferre...  33.2 us
  transfers between devices with their start and end apart: 4, of which 4 were waited for; matrix products, arithmetic and copies ran while one was open for 1% of the time, Pallas kernels for 0%

commit v1 on v0

v1 whole, which is shorter than its diff:
```python
import jax
import jax.numpy as jnp
from jax import lax
from jax.sharding import PartitionSpec as P


AXES = ("row", "col")


def bf16(value):
    return lax.reduce_precision(value, 8, 7).astype(jnp.bfloat16)


def body(inverse_tiles, factor, block_mask, diag_inverse):
    rows_here, cols_here = factor.shape
    width = diag_inverse.shape[1]
    sup_here = cols_here // width
    blocks_here = rows_here // width
    n_row, n_col = lax.axis_size("row"), lax.axis_size("col")
    ratio = n_row // n_col
    row_index = lax.axis_index("row")
    col_index = lax.axis_index("col")
    plane, part = row_index // ratio, row_index % ratio

    def send(value, target):
        pairs = []
        for row in range(n_row):
            for col in range(n_col):
                to_row, to_col = target(row, col)
                pairs.append((row * n_col + col, to_row * n_col + to_col))
        return lax.ppermute(value, AXES, pairs)

    def spread(step):
        return lambda row, col: ((col ^ step) * ratio + row % ratio, row // ratio)

    def swap(step):
        return lambda row, col: (row // ratio * ratio + (row + step) % ratio, col)

    def shift(step):
        return lambda row, col: (row, col ^ step)

    def flip(step):
        return lambda row, col: ((row // ratio ^ step) * ratio + row % ratio, col)

    mask_here = lax.dynamic_slice(
        block_mask, (row_index * blocks_here, col_index * sup_here), (blocks_here, sup_here)
    ).astype(jnp.bfloat16)
    blocks = factor.reshape(blocks_here, width, cols_here)

    own, gathered = [], []
    chunks = split(sup_here)
    for low, high in chunks:
        piece = blocks[:, :, low * width : high * width]
        keep = jnp.repeat(mask_here[:, low:high], width, 1)
        piece = (piece * keep[:, None, :]).reshape(rows_here, -1)
        own.append(piece)
        gathered.append([send(piece, spread(step)) for step in range(n_col)])

    parts = [
        lax.dynamic_slice_in_dim(inverse_tiles, (part + ratio - step) % ratio * rows_here, rows_here, 1)
        for step in range(ratio)
    ]

    def exchange(partial):
        partial = bf16(partial)
        pair = partial.astype(jnp.float32)
        for step in range(1, ratio):
            pair = pair + send(partial, swap(step)).astype(jnp.float32)
        pair = bf16(pair)
        terms = [pair] + [send(pair, flip(step)) for step in range(1, n_col)]
        terms = [t.astype(jnp.float32) for t in terms]
        while len(terms) > 1:
            terms = [terms[i] + terms[i + 1] for i in range(0, len(terms), 2)]
        return terms[0]

    own_diag = lax.dynamic_slice_in_dim(diag_inverse, col_index * sup_here, sup_here, 0)
    diag, off = [], []
    for chunk, (low, high) in enumerate(chunks):
        product = None
        for step in range(ratio):
            got = gathered[chunk]
            if step:
                got = [send(g, swap(step)) for g in got]
            term = lax.dot_general(
                jnp.concatenate(got, axis=1),
                parts[step],
                (((0,), (1,)), ((), ())),
                preferred_element_type=jnp.float32,
            )
            product = term if product is None else product + term
        product = product.reshape(n_col, -1, rows_here)
        slots = []
        for step in range(n_col):
            slots.append(
                lax.dynamic_index_in_dim(product, plane ^ col_index ^ step, 0, keepdims=False)
            )
        arrived = [send(slots[step].astype(jnp.bfloat16), shift(step)) for step in range(1, n_col)]
        total = slots[0]
        for value in arrived:
            total = total + value.astype(jnp.float32)
        off.append((-total).astype(jnp.bfloat16))
        low_total = total.astype(jnp.bfloat16)
        for sup in range(high - low):
            part_of = slice(sup * width, (sup + 1) * width)
            diag.append(
                lax.dot_general(
                    own[chunk][:, part_of],
                    low_total[part_of],
                    (((0,), (1,)), ((), ())),
                    preferred_element_type=jnp.float32,
                )
            )
    sums = []
    last = chunks[-1][0]
    if last:
        sums.append(exchange(jnp.stack(diag[:last])))
    sums.append(exchange(jnp.stack(diag[last:])))
    return jnp.concatenate(off, axis=0), own_diag + jnp.concatenate(sums)


def split(count):
    edges = list(range(count + 1))
    return list(zip(edges[:-1], edges[1:]))


def solution(mesh):
    return jax.shard_map(
        body,
        mesh=mesh,
        in_specs=(P("row", "col"), P("row", "col"), P(), P()),
        out_specs=(P("col", "row"), P("col", None, None)),
        check_vma=False,
    )
```

time: 571 us -> 296 us (0.52)
  waiting for transfers between devices: 499 us -> 74.9 us
  starting transfers between devices: 0.34 us -> 180 us
  between operations: 13.8 us -> 1.03 us
  other arithmetic: 14.9 us -> 6.35 us
    psum x2 -> x0, waiting for transfers between devices: 308 us -> none  [the longest x1 255 us: from_root(): return lax.psum(kept, axis)]
    ppermute x0 -> x52, starting transfers between devices: none -> 180 us  [send(): return lax.ppermute(value, AXES, pairs)]
    reduce_scatter x1 -> x0, waiting for transfers between devices: 118 us -> none  [per_device(): reduced = lax.psum_scatter(summed, 'col', scatter_dimension=0, tiled=True)]
    ppermute x0 -> x52, waiting for transfers between devices: none -> 74.9 us  [send(): return lax.ppermute(value, AXES, pairs)]
    all_gather x1 -> x0, waiting for transfers between devices: 72.7 us -> none  [per_device(): full_rows = lax.all_gather(masked, 'col', axis=1, tiled=True)]
    select_n x1 -> x0, other arithmetic: 8.13 us -> none  [from_root(): jnp.where(lax.axis_index(axis) == source, value, 0).astype(value.dtype)]
    dot_general x3 -> x12, matrix products: 38 us -> 32.5 us  [the longest x8 31.1 us: body(): lax.dot_general(jnp.concatenate(got, axis=1), parts[step], (((0,), (1,)),...]
  transfers between devices with their start and end apart: 4 -> 52, of which waited for: 4 -> 13; matrix products, arithmetic and copies ran while one was open for 1% -> 12% of each run, Pallas kernels for 0% -> 0%
where the time goes in v1:
time: 296 us
  starting transfers between devices  180 us (61%)
  waiting for transfers between devices  74.9 us (25%)
  matrix products  32.5 us (11%)
  other arithmetic  6.35 us (2%)
    ppermute x52, starting transfers between devices, send(): return lax.ppermute(value, AXES, pairs)  180 us
    ppermute x52, waiting for transfers between devices, send(): return lax.ppermute(value, AXES, pairs)  74.9 us
    dot_general x8, matrix products, body(): lax.dot_general(jnp.concatenate(got, axis=1), parts[step], (((0,), (1,)),...  31.1 us
  transfers between devices with their start and end apart: 52, of which 13 were waited for; matrix products, arithmetic and copies ran while one was open for 12% of the time, Pallas kernels for 0%

profile of v1, /device:TPU:0, one launch (start us, length us, event | category | flops | bytes accessed | tf_op | source)
XLA Modules:
  0.0 295.6 jit_solution(4378036679546162770)
XLA Ops:
  3.1 5.1 %collective-permute-start.14 = (bf16[1536,128]{1,0:T(8,128)(2,1)S(1)}, bf16[1536,128]{1,0:T(8,128)(2,1)}, u32[]{:S(2)}, u32[]{:S(2)}) collective-permute-start(bf16[1536,128]{1,0:T(8,128)(2,1)S(1)} %bitcast.125), channel_id=1, source_target_pairs={{0,24},{1,16},{2,8},{3,0},{4,28},{5,20},{6,12},{7,4},{8,25},{9,17}... | collective-permute-start | bytes 1179656 | tf_op jit(solution)/shard_map/ppermute | solution.py:31
  10.9 6.4 %collective-permute-start.36 = (bf16[1536,128]{1,0:T(8,128)(2,1)S(1)}, bf16[1536,128]{1,0:T(8,128)(2,1)S(1)}, u32[]{:S(2)}, u32[]{:S(2)}) collective-permute-start(bf16[1536,128]{1,0:T(8,128)(2,1)S(1)} %bitcast.110), channel_id=1, source_target_pairs={{0,24},{1,16},{2,8},{3,0},{4,28},{5,20},{6,12},{7,4},{8,25},{9,17}... | collective-permute-start | bytes 1179656 | tf_op jit(solution)/shard_map/ppermute | solution.py:31
  18.3 9.9 %collective-permute-start.35 = (bf16[1536,128]{1,0:T(8,128)(2,1)S(1)}, bf16[1536,128]{1,0:T(8,128)(2,1)S(1)}, u32[]{:S(2)}, u32[]{:S(2)}) collective-permute-start(bf16[1536,128]{1,0:T(8,128)(2,1)S(1)} %bitcast.111), channel_id=1, source_target_pairs={{0,16},{1,24},{2,0},{3,8},{4,20},{5,28},{6,4},{7,12},{8,17},{9,25}... | collective-permute-start | bytes 1179656 | tf_op jit(solution)/shard_map/ppermute | solution.py:31
  28.2 5.4 %collective-permute-done.13 = bf16[1536,128]{1,0:T(8,128)(2,1)} collective-permute-done((bf16[1536,128]{1,0:T(8,128)(2,1)S(1)}, bf16[1536,128]{1,0:T(8,128)(2,1)}, u32[]{:S(2)}, u32[]{:S(2)}) %collective-permute-start.13) | collective-permute-done | bytes 393248 | tf_op jit(solution)/shard_map/ppermute | solution.py:31
  33.6 27.8 %collective-permute-start.34 = (bf16[1536,128]{1,0:T(8,128)(2,1)S(1)}, bf16[1536,128]{1,0:T(8,128)(2,1)S(1)}, u32[]{:S(2)}, u32[]{:S(2)}) collective-permute-start(bf16[1536,128]{1,0:T(8,128)(2,1)S(1)} %bitcast.112), channel_id=1, source_target_pairs={{0,8},{1,0},{2,24},{3,16},{4,12},{5,4},{6,28},{7,20},{8,9},{9,1},{... | collective-permute-start | bytes 1179656 | tf_op jit(solution)/shard_map/ppermute | solution.py:31
  62.2 5.0 %fusion.8 = f32[512,1536]{1,0:T(8,128)S(1)} fusion(bf16[1536,3072]{1,0:T(8,128)(2,1)} %param.4, s32[]{:T(128)S(6)} %select_n.61, bf16[1536,128]{1,0:T(8,128)(2,1)} %collective-permute-done.14, bf16[1536,128]{1,0:T(8,128)(2,1)} %collective-permute-done.13, bf16[1536,128]{1,0:T(8,128)(2,1)} %collective-permute-done.12, ...), kind=kOutput, calls=%fused_computation.12 | convolution fusion | flops 2422210560 | bytes 9437188 | tf_op jit(solution)/shard_map/dot_general | solution.py:84
  67.2 6.6 %collective-permute-start.24 = (bf16[1536,128]{1,0:T(8,128)(2,1)S(1)}, bf16[1536,128]{1,0:T(8,128)(2,1)S(1)}, u32[]{:S(2)}, u32[]{:S(2)}) collective-permute-start(bf16[1536,128]{1,0:T(8,128)(2,1)S(1)} %bitcast.121), channel_id=1, source_target_pairs={{0,16},{1,24},{2,0},{3,8},{4,20},{5,28},{6,4},{7,12},{8,17},{9,25}... | collective-permute-start | bytes 1179656 | tf_op jit(solution)/shard_map/ppermute | solution.py:31
  73.9 24.3 %collective-permute-start.23 = (bf16[1536,128]{1,0:T(8,128)(2,1)S(1)}, bf16[1536,128]{1,0:T(8,128)(2,1)S(1)}, u32[]{:S(2)}, u32[]{:S(2)}) collective-permute-start(bf16[1536,128]{1,0:T(8,128)(2,1)S(1)} %bitcast.122), channel_id=1, source_target_pairs={{0,8},{1,0},{2,24},{3,16},{4,12},{5,4},{6,28},{7,20},{8,9},{9,1},{... | collective-permute-start | bytes 1179656 | tf_op jit(solution)/shard_map/ppermute | solution.py:31
  99.0 2.7 fusion.4
  101.7 4.9 %collective-permute-start.2 = (bf16[1536,128]{1,0:T(8,128)(2,1)S(1)}, bf16[1536,128]{1,0:T(8,128)(2,1)S(1)}, u32[]{:S(2)}, u32[]{:S(2)}) collective-permute-start(bf16[1536,128]{1,0:T(8,128)(2,1)S(1)} %bitcast.116), channel_id=1, source_target_pairs={{0,16},{1,24},{2,0},{3,8},{4,20},{5,28},{6,4},{7,12},{8,17},{9,25}... | collective-permute-start | bytes 1179656 | tf_op jit(solution)/shard_map/ppermute | solution.py:31
  106.6 25.4 %collective-permute-start.1 = (bf16[1536,128]{1,0:T(8,128)(2,1)S(1)}, bf16[1536,128]{1,0:T(8,128)(2,1)S(1)}, u32[]{:S(2)}, u32[]{:S(2)}) collective-permute-start(bf16[1536,128]{1,0:T(8,128)(2,1)S(1)} %bitcast.117), channel_id=1, source_target_pairs={{0,8},{1,0},{2,24},{3,16},{4,12},{5,4},{6,28},{7,20},{8,9},{9,1},{... | collective-permute-start | bytes 1179656 | tf_op jit(solution)/shard_map/ppermute | solution.py:31
  132.9 4.3 %fusion.6 = f32[512,1536]{1,0:T(8,128)} fusion(bf16[1536,3072]{1,0:T(8,128)(2,1)S(1)} %bitcast.131, s32[]{:T(128)S(6)} %select_n.61, bf16[1536,128]{1,0:T(8,128)(2,1)S(1)} %collective-permute-done.25, bf16[1536,128]{1,0:T(8,128)(2,1)S(1)} %collective-permute-done.24, bf16[1536,128]{1,0:T(8,128)(2,1)S(1)} %collective-permute-done.23, ...), kind=kOutput, calls=%fused_computation.10 | convolution fusion | flops 2422210560 | bytes 9437188 | tf_op jit(solution)/shard_map/dot_general | solution.py:84
  137.8 2.7 collective-permute-done.1
  140.9 4.4 %fusion.10 = f32[512,1536]{1,0:T(8,128)} fusion(bf16[1536,3072]{1,0:T(8,128)(2,1)S(1)} %bitcast.131, s32[]{:T(128)S(6)} %select_n.61, bf16[1536,128]{1,0:T(8,128)(2,1)S(1)} %collective-permute-done.3, bf16[1536,128]{1,0:T(8,128)(2,1)S(1)} %collective-permute-done.2, bf16[1536,128]{1,0:T(8,128)(2,1)S(1)} %collective-permute-done.1, ...), kind=kOutput, calls=%fused_computation.14 | convolution fusion | flops 2422210560 | bytes 9437188 | tf_op jit(solution)/shard_map/dot_general | solution.py:84
  146.4 2.6 convolution_add_fusion.2
  150.1 4.6 %convolution_add_fusion.1 = f32[512,1536]{1,0:T(8,128)S(1)} fusion(f32[512,1536]{1,0:T(8,128)} %fusion.6, bf16[1536,3072]{1,0:T(8,128)(2,1)S(1)} %bitcast.131, s32[]{:T(128)S(6)} %select_n.63, bf16[1536,128]{1,0:T(8,128)(2,1)S(1)} %collective-permute-done.29, bf16[1536,128]{1,0:T(8,128)(2,1)S(1)} %collective-permute-done.28, ...), kind=kOutput, calls=%fused_computation.1 | convolution fusion | flops 2422996992 | bytes 12582916 | tf_op jit(solution)/shard_map/dot_general | solution.py:84
  155.6 14.9 %collective-permute-start.19 = (bf16[128,1536]{1,0:T(8,128)(2,1)S(1)}, bf16[128,1536]{1,0:T(8,128)(2,1)S(1)}, u32[]{:S(2)}, u32[]{:S(2)}) collective-permute-start(bf16[128,1536]{1,0:T(8,128)(2,1)S(1)} %get-tuple-element.5), channel_id=1, source_target_pairs={{0,1},{1,0},{2,3},{3,2},{4,5},{5,4},{6,7},{7,6},{8,9},{9,8},{10,11... | collective-permute-start | bytes 1179656 | tf_op jit(solution)/shard_map/ppermute | solution.py:31
  170.6 4.8 %convolution_add_fusion.3 = f32[512,1536]{1,0:T(8,128)S(1)} fusion(f32[512,1536]{1,0:T(8,128)} %fusion.10, bf16[1536,3072]{1,0:T(8,128)(2,1)S(1)} %bitcast.131, s32[]{:T(128)S(6)} %select_n.63, bf16[1536,128]{1,0:T(8,128)(2,1)S(1)} %collective-permute-done.7, bf16[1536,128]{1,0:T(8,128)(2,1)S(1)} %collective-permute-done.6, ...), kind=kOutput, calls=%fused_computation.3 | convolution fusion | flops 2422996992 | bytes 12582916 | tf_op jit(solution)/shard_map/dot_general | solution.py:84
  175.5 24.9 %collective-permute-start.21 = (bf16[128,1536]{1,0:T(8,128)(2,1)S(1)}, bf16[128,1536]{1,0:T(8,128)(2,1)S(1)}, u32[]{:S(2)}, u32[]{:S(2)}) collective-permute-start(bf16[128,1536]{1,0:T(8,128)(2,1)S(1)} %get-tuple-element.6), channel_id=1, source_target_pairs={{0,3},{1,2},{2,1},{3,0},{4,7},{5,6},{6,5},{7,4},{8,11},{9,10},{10,... | collective-permute-start | bytes 1179656 | tf_op jit(solution)/shard_map/ppermute | solution.py:31
  201.1 2.8 collective-permute-start.32
  204.0 2.6 convolution_add_fusion
  206.9 6.9 %collective-permute-done.21 = bf16[128,1536]{1,0:T(8,128)(2,1)S(1)} collective-permute-done((bf16[128,1536]{1,0:T(8,128)(2,1)S(1)}, bf16[128,1536]{1,0:T(8,128)(2,1)S(1)}, u32[]{:S(2)}, u32[]{:S(2)}) %collective-permute-start.21) | collective-permute-done | bytes 393248 | tf_op jit(solution)/shard_map/ppermute | solution.py:31
  213.9 7.0 %collective-permute-done.20 = bf16[128,1536]{1,0:T(8,128)(2,1)S(1)} collective-permute-done((bf16[128,1536]{1,0:T(8,128)(2,1)S(1)}, bf16[128,1536]{1,0:T(8,128)(2,1)S(1)}, u32[]{:S(2)}, u32[]{:S(2)}) %collective-permute-start.20) | collective-permute-done | bytes 393248 | tf_op jit(solution)/shard_map/ppermute | solution.py:31
  223.3 7.4 %collective-permute-done.32 = bf16[128,1536]{1,0:T(8,128)(2,1)S(1)} collective-permute-done((bf16[128,1536]{1,0:T(8,128)(2,1)S(1)}, bf16[128,1536]{1,0:T(8,128)(2,1)S(1)}, u32[]{:S(2)}, u32[]{:S(2)}) %collective-permute-start.32) | collective-permute-done | bytes 393248 | tf_op jit(solution)/shard_map/ppermute | solution.py:31
  230.8 7.0 %collective-permute-done.31 = bf16[128,1536]{1,0:T(8,128)(2,1)S(1)} collective-permute-done((bf16[128,1536]{1,0:T(8,128)(2,1)S(1)}, bf16[128,1536]{1,0:T(8,128)(2,1)S(1)}, u32[]{:S(2)}, u32[]{:S(2)}) %collective-permute-start.31) | collective-permute-done | bytes 393248 | tf_op jit(solution)/shard_map/ppermute | solution.py:31
  240.1 7.6 %collective-permute-done.10 = bf16[128,1536]{1,0:T(8,128)(2,1)S(1)} collective-permute-done((bf16[128,1536]{1,0:T(8,128)(2,1)S(1)}, bf16[128,1536]{1,0:T(8,128)(2,1)S(1)}, u32[]{:S(2)}, u32[]{:S(2)}) %collective-permute-start.10) | collective-permute-done | bytes 393248 | tf_op jit(solution)/shard_map/ppermute | solution.py:31
  247.7 6.9 %collective-permute-done.9 = bf16[128,1536]{1,0:T(8,128)(2,1)S(1)} collective-permute-done((bf16[128,1536]{1,0:T(8,128)(2,1)S(1)}, bf16[128,1536]{1,0:T(8,128)(2,1)S(1)}, u32[]{:S(2)}, u32[]{:S(2)}) %collective-permute-start.9) | collective-permute-done | bytes 393248 | tf_op jit(solution)/shard_map/ppermute | solution.py:31
  255.1 8.9 %collective-permute-done.43 = bf16[128,1536]{1,0:T(8,128)(2,1)S(1)} collective-permute-done((bf16[128,1536]{1,0:T(8,128)(2,1)S(1)}, bf16[128,1536]{1,0:T(8,128)(2,1)S(1)}, u32[]{:S(2)}, u32[]{:S(2)}) %collective-permute-start.43) | collective-permute-done | bytes 393248 | tf_op jit(solution)/shard_map/ppermute | solution.py:31
  264.0 6.3 %collective-permute-done.42 = bf16[128,1536]{1,0:T(8,128)(2,1)S(1)} collective-permute-done((bf16[128,1536]{1,0:T(8,128)(2,1)S(1)}, bf16[128,1536]{1,0:T(8,128)(2,1)S(1)}, u32[]{:S(2)}, u32[]{:S(2)}) %collective-permute-start.42) | collective-permute-done | bytes 393248 | tf_op jit(solution)/shard_map/ppermute | solution.py:31
  273.0 8.6 %collective-permute-start.50 = (bf16[1,128,128]{2,1,0:T(8,128)(2,1)S(1)}, bf16[1,128,128]{2,1,0:T(8,128)(2,1)S(1)}, u32[]{:S(2)}, u32[]{:S(2)}) collective-permute-start(bf16[1,128,128]{2,1,0:T(8,128)(2,1)S(1)} %reduce-precision_convert_fusion.1), channel_id=1, source_target_pairs={{0,16},{1,17},{2,18},{3,19},{4,20},{5,21},{6,22},{7,23},{8,24},{9,... | collective-permute-start | bytes 98312 | tf_op jit(solution)/shard_map/ppermute | solution.py:31
  286.1 3.1 %collective-permute-done.47 = bf16[3,128,128]{2,1,0:T(8,128)(2,1)S(1)} collective-permute-done((bf16[3,128,128]{2,1,0:T(8,128)(2,1)S(1)}, bf16[3,128,128]{2,1,0:T(8,128)(2,1)S(1)}, u32[]{:S(2)}, u32[]{:S(2)}) %collective-permute-start.47) | collective-permute-done | bytes 98336 | tf_op jit(solution)/shard_map/ppermute | solution.py:31
  289.2 4.6 %collective-permute-done.46 = bf16[3,128,128]{2,1,0:T(8,128)(2,1)S(1)} collective-permute-done((bf16[3,128,128]{2,1,0:T(8,128)(2,1)S(1)}, bf16[3,128,128]{2,1,0:T(8,128)(2,1)S(1)}, u32[]{:S(2)}, u32[]{:S(2)}) %collective-permute-start.46) | collective-permute-done | bytes 98336 | tf_op jit(solution)/shard_map/ppermute | solution.py:31
  (109 shorter events, 27.8 us)
Async XLA Ops:
  3.1 15.2 %collective-permute-start.14 = (bf16[1536,128]{1,0:T(8,128)(2,1)S(1)}, bf16[1536,128]{1,0:T(8,128)(2,1)}, u32[]{:S(2)}, u32[]{:S(2)}) collective-permute-start(bf16[1536,128]{1,0:T(8,128)(2,1)S(1)} %bitcast.125), channel_id=1, source_target_pairs={{0,24},{1,16},{2,8},{3,0},{4,28},{5,20},{6,12},{7,4},{8,25},{9,17}... | collective-permute-start | bytes 1179656 | tf_op jit(solution)/shard_map/ppermute | solution.py:31
  8.2 25.4 %collective-permute-start.13 = (bf16[1536,128]{1,0:T(8,128)(2,1)S(1)}, bf16[1536,128]{1,0:T(8,128)(2,1)}, u32[]{:S(2)}, u32[]{:S(2)}) collective-permute-start(bf16[1536,128]{1,0:T(8,128)(2,1)S(1)} %bitcast.126), channel_id=1, source_target_pairs={{0,16},{1,24},{2,0},{3,8},{4,20},{5,28},{6,4},{7,12},{8,17},{9,25}... | collective-permute-start | bytes 1179656 | tf_op jit(solution)/shard_map/ppermute | solution.py:31
  9.7 51.7 %collective-permute-start.12 = (bf16[1536,128]{1,0:T(8,128)(2,1)S(1)}, bf16[1536,128]{1,0:T(8,128)(2,1)}, u32[]{:S(2)}, u32[]{:S(2)}) collective-permute-start(bf16[1536,128]{1,0:T(8,128)(2,1)S(1)} %bitcast.127), channel_id=1, source_target_pairs={{0,8},{1,0},{2,24},{3,16},{4,12},{5,4},{6,28},{7,20},{8,9},{9,1},{... | collective-permute-start | bytes 1179656 | tf_op jit(solution)/shard_map/ppermute | solution.py:31
  10.2 51.9 %collective-permute-start.11 = (bf16[1536,128]{1,0:T(8,128)(2,1)S(1)}, bf16[1536,128]{1,0:T(8,128)(2,1)S(1)}, u32[]{:S(2)}, u32[]{:S(2)}) collective-permute-start(bf16[1536,128]{1,0:T(8,128)(2,1)S(1)} %bitcast.128), channel_id=1, source_target_pairs={{0,0},{1,8},{2,16},{3,24},{4,4},{5,12},{6,20},{7,28},{8,1},{9,9},{... | collective-permute-start | bytes 1179656 | tf_op jit(solution)/shard_map/ppermute | solution.py:31
  10.9 56.4 %collective-permute-start.36 = (bf16[1536,128]{1,0:T(8,128)(2,1)S(1)}, bf16[1536,128]{1,0:T(8,128)(2,1)S(1)}, u32[]{:S(2)}, u32[]{:S(2)}) collective-permute-start(bf16[1536,128]{1,0:T(8,128)(2,1)S(1)} %bitcast.110), channel_id=1, source_target_pairs={{0,24},{1,16},{2,8},{3,0},{4,28},{5,20},{6,12},{7,4},{8,25},{9,17}... | collective-permute-start | bytes 1179656 | tf_op jit(solution)/shard_map/ppermute | solution.py:31
  18.3 55.6 %collective-permute-start.35 = (bf16[1536,128]{1,0:T(8,128)(2,1)S(1)}, bf16[1536,128]{1,0:T(8,128)(2,1)S(1)}, u32[]{:S(2)}, u32[]{:S(2)}) collective-permute-start(bf16[1536,128]{1,0:T(8,128)(2,1)S(1)} %bitcast.111), channel_id=1, source_target_pairs={{0,16},{1,24},{2,0},{3,8},{4,20},{5,28},{6,4},{7,12},{8,17},{9,25}... | collective-permute-start | bytes 1179656 | tf_op jit(solution)/shard_map/ppermute | solution.py:31
  33.6 64.6 %collective-permute-start.34 = (bf16[1536,128]{1,0:T(8,128)(2,1)S(1)}, bf16[1536,128]{1,0:T(8,128)(2,1)S(1)}, u32[]{:S(2)}, u32[]{:S(2)}) collective-permute-start(bf16[1536,128]{1,0:T(8,128)(2,1)S(1)} %bitcast.112), channel_id=1, source_target_pairs={{0,8},{1,0},{2,24},{3,16},{4,12},{5,4},{6,28},{7,20},{8,9},{9,1},{... | collective-permute-start | bytes 1179656 | tf_op jit(solution)/shard_map/ppermute | solution.py:31
  61.4 37.5 %collective-permute-start.33 = (bf16[1536,128]{1,0:T(8,128)(2,1)S(1)}, bf16[1536,128]{1,0:T(8,128)(2,1)S(1)}, u32[]{:S(2)}, u32[]{:S(2)}) collective-permute-start(bf16[1536,128]{1,0:T(8,128)(2,1)S(1)} %bitcast.113), channel_id=1, source_target_pairs={{0,0},{1,8},{2,16},{3,24},{4,4},{5,12},{6,20},{7,28},{8,1},{9,9},{... | collective-permute-start | bytes 1179656 | tf_op jit(solution)/shard_map/ppermute | solution.py:31
  62.1 39.5 %collective-permute-start.25 = (bf16[1536,128]{1,0:T(8,128)(2,1)S(1)}, bf16[1536,128]{1,0:T(8,128)(2,1)S(1)}, u32[]{:S(2)}, u32[]{:S(2)}) collective-permute-start(bf16[1536,128]{1,0:T(8,128)(2,1)S(1)} %bitcast.120), channel_id=1, source_target_pairs={{0,24},{1,16},{2,8},{3,0},{4,28},{5,20},{6,12},{7,4},{8,25},{9,17}... | collective-permute-start | bytes 1179656 | tf_op jit(solution)/shard_map/ppermute | solution.py:31
  67.2 39.4 %collective-permute-start.24 = (bf16[1536,128]{1,0:T(8,128)(2,1)S(1)}, bf16[1536,128]{1,0:T(8,128)(2,1)S(1)}, u32[]{:S(2)}, u32[]{:S(2)}) collective-permute-start(bf16[1536,128]{1,0:T(8,128)(2,1)S(1)} %bitcast.121), channel_id=1, source_target_pairs={{0,16},{1,24},{2,0},{3,8},{4,20},{5,28},{6,4},{7,12},{8,17},{9,25}... | collective-permute-start | bytes 1179656 | tf_op jit(solution)/shard_map/ppermute | solution.py:31
  73.9 58.1 %collective-permute-start.23 = (bf16[1536,128]{1,0:T(8,128)(2,1)S(1)}, bf16[1536,128]{1,0:T(8,128)(2,1)S(1)}, u32[]{:S(2)}, u32[]{:S(2)}) collective-permute-start(bf16[1536,128]{1,0:T(8,128)(2,1)S(1)} %bitcast.122), channel_id=1, source_target_pairs={{0,8},{1,0},{2,24},{3,16},{4,12},{5,4},{6,28},{7,20},{8,9},{9,1},{... | collective-permute-start | bytes 1179656 | tf_op jit(solution)/shard_map/ppermute | solution.py:31
  98.2 34.7 %collective-permute-start.22 = (bf16[1536,128]{1,0:T(8,128)(2,1)S(1)}, bf16[1536,128]{1,0:T(8,128)(2,1)S(1)}, u32[]{:S(2)}, u32[]{:S(2)}) collective-permute-start(bf16[1536,128]{1,0:T(8,128)(2,1)S(1)} %bitcast.123), channel_id=1, source_target_pairs={{0,0},{1,8},{2,16},{3,24},{4,4},{5,12},{6,20},{7,28},{8,1},{9,9},{... | collective-permute-start | bytes 1179656 | tf_op jit(solution)/shard_map/ppermute | solution.py:31
  98.9 38.4 %collective-permute-start.3 = (bf16[1536,128]{1,0:T(8,128)(2,1)S(1)}, bf16[1536,128]{1,0:T(8,128)(2,1)S(1)}, u32[]{:S(2)}, u32[]{:S(2)}) collective-permute-start(bf16[1536,128]{1,0:T(8,128)(2,1)S(1)} %bitcast.115), channel_id=1, source_target_pairs={{0,24},{1,16},{2,8},{3,0},{4,28},{5,20},{6,12},{7,4},{8,25},{9,17}... | collective-permute-start | bytes 1179656 | tf_op jit(solution)/shard_map/ppermute | solution.py:31
  101.7 36.0 %collective-permute-start.2 = (bf16[1536,128]{1,0:T(8,128)(2,1)S(1)}, bf16[1536,128]{1,0:T(8,128)(2,1)S(1)}, u32[]{:S(2)}, u32[]{:S(2)}) collective-permute-start(bf16[1536,128]{1,0:T(8,128)(2,1)S(1)} %bitcast.116), channel_id=1, source_target_pairs={{0,16},{1,24},{2,0},{3,8},{4,20},{5,28},{6,4},{7,12},{8,17},{9,25}... | collective-permute-start | bytes 1179656 | tf_op jit(solution)/shard_map/ppermute | solution.py:31
  106.6 33.8 %collective-permute-start.1 = (bf16[1536,128]{1,0:T(8,128)(2,1)S(1)}, bf16[1536,128]{1,0:T(8,128)(2,1)S(1)}, u32[]{:S(2)}, u32[]{:S(2)}) collective-permute-start(bf16[1536,128]{1,0:T(8,128)(2,1)S(1)} %bitcast.117), channel_id=1, source_target_pairs={{0,8},{1,0},{2,24},{3,16},{4,12},{5,4},{6,28},{7,20},{8,9},{9,1},{... | collective-permute-start | bytes 1179656 | tf_op jit(solution)/shard_map/ppermute | solution.py:31
  132.8 42.7 %collective-permute-start.40 = (bf16[1536,128]{1,0:T(8,128)(2,1)S(1)}, bf16[1536,128]{1,0:T(8,128)(2,1)S(1)}, u32[]{:S(2)}, u32[]{:S(2)}) collective-permute-start(bf16[1536,128]{1,0:T(8,128)(2,1)S(1)} %collective-permute-done.36), channel_id=1, source_target_pairs={{0,4},{1,5},{2,6},{3,7},{4,0},{5,1},{6,2},{7,3},{8,12},{9,13},{10,... | collective-permute-start | bytes 1179656 | tf_op jit(solution)/shard_map/ppermute | solution.py:31
  154.9 45.6 %collective-permute-start.39 = (bf16[1536,128]{1,0:T(8,128)(2,1)S(1)}, bf16[1536,128]{1,0:T(8,128)(2,1)S(1)}, u32[]{:S(2)}, u32[]{:S(2)}) collective-permute-start(bf16[1536,128]{1,0:T(8,128)(2,1)S(1)} %collective-permute-done.35), channel_id=1, source_target_pairs={{0,4},{1,5},{2,6},{3,7},{4,0},{5,1},{6,2},{7,3},{8,12},{9,13},{10,... | collective-permute-start | bytes 1179656 | tf_op jit(solution)/shard_map/ppermute | solution.py:31
  155.1 45.4 %collective-permute-start.38 = (bf16[1536,128]{1,0:T(8,128)(2,1)S(1)}, bf16[1536,128]{1,0:T(8,128)(2,1)S(1)}, u32[]{:S(2)}, u32[]{:S(2)}) collective-permute-start(bf16[1536,128]{1,0:T(8,128)(2,1)S(1)} %collective-permute-done.34), channel_id=1, source_target_pairs={{0,4},{1,5},{2,6},{3,7},{4,0},{5,1},{6,2},{7,3},{8,12},{9,13},{10,... | collective-permute-start | bytes 1179656 | tf_op jit(solution)/shard_map/ppermute | solution.py:31
  155.4 45.7 %collective-permute-start.37 = (bf16[1536,128]{1,0:T(8,128)(2,1)S(1)}, bf16[1536,128]{1,0:T(8,128)(2,1)S(1)}, u32[]{:S(2)}, u32[]{:S(2)}) collective-permute-start(bf16[1536,128]{1,0:T(8,128)(2,1)S(1)} %collective-permute-done.33), channel_id=1, source_target_pairs={{0,4},{1,5},{2,6},{3,7},{4,0},{5,1},{6,2},{7,3},{8,12},{9,13},{10,... | collective-permute-start | bytes 1179656 | tf_op jit(solution)/shard_map/ppermute | solution.py:31
  155.6 51.2 %collective-permute-start.19 = (bf16[128,1536]{1,0:T(8,128)(2,1)S(1)}, bf16[128,1536]{1,0:T(8,128)(2,1)S(1)}, u32[]{:S(2)}, u32[]{:S(2)}) collective-permute-start(bf16[128,1536]{1,0:T(8,128)(2,1)S(1)} %get-tuple-element.5), channel_id=1, source_target_pairs={{0,1},{1,0},{2,3},{3,2},{4,5},{5,4},{6,7},{7,6},{8,9},{9,8},{10,11... | collective-permute-start | bytes 1179656 | tf_op jit(solution)/shard_map/ppermute | solution.py:31
  175.5 38.3 %collective-permute-start.21 = (bf16[128,1536]{1,0:T(8,128)(2,1)S(1)}, bf16[128,1536]{1,0:T(8,128)(2,1)S(1)}, u32[]{:S(2)}, u32[]{:S(2)}) collective-permute-start(bf16[128,1536]{1,0:T(8,128)(2,1)S(1)} %get-tuple-element.6), channel_id=1, source_target_pairs={{0,3},{1,2},{2,1},{3,0},{4,7},{5,6},{6,5},{7,4},{8,11},{9,10},{10,... | collective-permute-start | bytes 1179656 | tf_op jit(solution)/shard_map/ppermute | solution.py:31
  200.5 20.4 %collective-permute-start.20 = (bf16[128,1536]{1,0:T(8,128)(2,1)S(1)}, bf16[128,1536]{1,0:T(8,128)(2,1)S(1)}, u32[]{:S(2)}, u32[]{:S(2)}) collective-permute-start(bf16[128,1536]{1,0:T(8,128)(2,1)S(1)} %get-tuple-element.7), channel_id=1, source_target_pairs={{0,2},{1,3},{2,0},{3,1},{4,6},{5,7},{6,4},{7,5},{8,10},{9,11},{10,... | collective-permute-start | bytes 1179656 | tf_op jit(solution)/shard_map/ppermute | solution.py:31
  200.5 21.4 %collective-permute-start.30 = (bf16[128,1536]{1,0:T(8,128)(2,1)S(1)}, bf16[128,1536]{1,0:T(8,128)(2,1)S(1)}, u32[]{:S(2)}, u32[]{:S(2)}) collective-permute-start(bf16[128,1536]{1,0:T(8,128)(2,1)S(1)} %get-tuple-element.8), channel_id=1, source_target_pairs={{0,1},{1,0},{2,3},{3,2},{4,5},{5,4},{6,7},{7,6},{8,9},{9,8},{10,11... | collective-permute-start | bytes 1179656 | tf_op jit(solution)/shard_map/ppermute | solution.py:31
  201.1 29.6 %collective-permute-start.32 = (bf16[128,1536]{1,0:T(8,128)(2,1)S(1)}, bf16[128,1536]{1,0:T(8,128)(2,1)S(1)}, u32[]{:S(2)}, u32[]{:S(2)}) collective-permute-start(bf16[128,1536]{1,0:T(8,128)(2,1)S(1)} %get-tuple-element.9), channel_id=1, source_target_pairs={{0,3},{1,2},{2,1},{3,0},{4,7},{5,6},{6,5},{7,4},{8,11},{9,10},{10,... | collective-permute-start | bytes 1179656 | tf_op jit(solution)/shard_map/ppermute | solution.py:31
  206.8 31.0 %collective-permute-start.31 = (bf16[128,1536]{1,0:T(8,128)(2,1)S(1)}, bf16[128,1536]{1,0:T(8,128)(2,1)S(1)}, u32[]{:S(2)}, u32[]{:S(2)}) collective-permute-start(bf16[128,1536]{1,0:T(8,128)(2,1)S(1)} %get-tuple-element.10), channel_id=1, source_target_pairs={{0,2},{1,3},{2,0},{3,1},{4,6},{5,7},{6,4},{7,5},{8,10},{9,11},{10,... | collective-permute-start | bytes 1179656 | tf_op jit(solution)/shard_map/ppermute | solution.py:31
  213.9 24.8 %collective-permute-start.8 = (bf16[128,1536]{1,0:T(8,128)(2,1)S(1)}, bf16[128,1536]{1,0:T(8,128)(2,1)S(1)}, u32[]{:S(2)}, u32[]{:S(2)}) collective-permute-start(bf16[128,1536]{1,0:T(8,128)(2,1)S(1)} %get-tuple-element.2), channel_id=1, source_target_pairs={{0,1},{1,0},{2,3},{3,2},{4,5},{5,4},{6,7},{7,6},{8,9},{9,8},{10,11... | collective-permute-start | bytes 1179656 | tf_op jit(solution)/shard_map/ppermute | solution.py:31
  220.9 26.8 %collective-permute-start.10 = (bf16[128,1536]{1,0:T(8,128)(2,1)S(1)}, bf16[128,1536]{1,0:T(8,128)(2,1)S(1)}, u32[]{:S(2)}, u32[]{:S(2)}) collective-permute-start(bf16[128,1536]{1,0:T(8,128)(2,1)S(1)} %get-tuple-element.3), channel_id=1, source_target_pairs={{0,3},{1,2},{2,1},{3,0},{4,7},{5,6},{6,5},{7,4},{8,11},{9,10},{10,... | collective-permute-start | bytes 1179656 | tf_op jit(solution)/shard_map/ppermute | solution.py:31
  221.9 32.7 %collective-permute-start.9 = (bf16[128,1536]{1,0:T(8,128)(2,1)S(1)}, bf16[128,1536]{1,0:T(8,128)(2,1)S(1)}, u32[]{:S(2)}, u32[]{:S(2)}) collective-permute-start(bf16[128,1536]{1,0:T(8,128)(2,1)S(1)} %get-tuple-element.4), channel_id=1, source_target_pairs={{0,2},{1,3},{2,0},{3,1},{4,6},{5,7},{6,4},{7,5},{8,10},{9,11},{10,... | collective-permute-start | bytes 1179656 | tf_op jit(solution)/shard_map/ppermute | solution.py:31
  230.8 24.3 %collective-permute-start.41 = (bf16[128,1536]{1,0:T(8,128)(2,1)S(1)}, bf16[128,1536]{1,0:T(8,128)(2,1)S(1)}, u32[]{:S(2)}, u32[]{:S(2)}) collective-permute-start(bf16[128,1536]{1,0:T(8,128)(2,1)S(1)} %get-tuple-element.11), channel_id=1, source_target_pairs={{0,1},{1,0},{2,3},{3,2},{4,5},{5,4},{6,7},{7,6},{8,9},{9,8},{10,11... | collective-permute-start | bytes 1179656 | tf_op jit(solution)/shard_map/ppermute | solution.py:31
  237.8 26.2 %collective-permute-start.43 = (bf16[128,1536]{1,0:T(8,128)(2,1)S(1)}, bf16[128,1536]{1,0:T(8,128)(2,1)S(1)}, u32[]{:S(2)}, u32[]{:S(2)}) collective-permute-start(bf16[128,1536]{1,0:T(8,128)(2,1)S(1)} %get-tuple-element.12), channel_id=1, source_target_pairs={{0,3},{1,2},{2,1},{3,0},{4,7},{5,6},{6,5},{7,4},{8,11},{9,10},{10,... | collective-permute-start | bytes 1179656 | tf_op jit(solution)/shard_map/ppermute | solution.py:31
  238.7 31.6 %collective-permute-start.42 = (bf16[128,1536]{1,0:T(8,128)(2,1)S(1)}, bf16[128,1536]{1,0:T(8,128)(2,1)S(1)}, u32[]{:S(2)}, u32[]{:S(2)}) collective-permute-start(bf16[128,1536]{1,0:T(8,128)(2,1)S(1)} %get-tuple-element.13), channel_id=1, source_target_pairs={{0,2},{1,3},{2,0},{3,1},{4,6},{5,7},{6,4},{7,5},{8,10},{9,11},{10,... | collective-permute-start | bytes 1179656 | tf_op jit(solution)/shard_map/ppermute | solution.py:31
  255.0 26.6 %collective-permute-start.44 = (bf16[3,128,128]{2,1,0:T(8,128)(2,1)S(1)}, bf16[3,128,128]{2,1,0:T(8,128)(2,1)S(1)}, u32[]{:S(2)}, u32[]{:S(2)}) collective-permute-start(bf16[3,128,128]{2,1,0:T(8,128)(2,1)S(1)} %fusion.94), channel_id=1, source_target_pairs={{0,4},{1,5},{2,6},{3,7},{4,0},{5,1},{6,2},{7,3},{8,12},{9,13},{10,... | collective-permute-start | bytes 294920 | tf_op jit(solution)/shard_map/ppermute | solution.py:31
  (23 other events, 303.9 us)

commit v2 on v1

--- a/solution.py
+++ b/solution.py
@@ -115,7 +115,12 @@
     if last:
         sums.append(exchange(jnp.stack(diag[:last])))
     sums.append(exchange(jnp.stack(diag[last:])))
-    return jnp.concatenate(off, axis=0), own_diag + jnp.concatenate(sums)
+    done = jnp.concatenate(off, axis=0)
+    if not last:
+        return done, own_diag + sums[0]
+    base = jnp.concatenate([own_diag[:last] + sums[0], own_diag[last:]])
+    base = lax.optimization_barrier(base)
+    return done, lax.dynamic_update_slice_in_dim(base, base[last:] + sums[1], last, 0)
 
 
 def split(count):

time: 296 us -> 293 us (0.990)
  waiting for transfers between devices: 74.9 us -> 69.3 us
    ppermute x52, waiting for transfers between devices: 74.9 us -> 69.3 us  [send(): return lax.ppermute(value, AXES, pairs)]
  transfers between devices with their start and end apart: 52 -> 52, of which waited for: 13 -> 12; matrix products, arithmetic and copies ran while one was open for 12% -> 13% of each run, Pallas kernels for 0% -> 0%
where the time goes in v2:
time: 293 us
  starting transfers between devices  182 us (62%)
  waiting for transfers between devices  69.3 us (24%)
  matrix products  32.6 us (11%)
  other arithmetic  5.64 us (2%)
    ppermute x52, starting transfers between devices, send(): return lax.ppermute(value, AXES, pairs)  182 us
    ppermute x52, waiting for transfers between devices, send(): return lax.ppermute(value, AXES, pairs)  69.3 us
    dot_general x8, matrix products, body(): lax.dot_general(jnp.concatenate(got, axis=1), parts[step], (((0,), (1,)),...  31.1 us
  transfers between devices with their start and end apart: 52, of which 12 were waited for; matrix products, arithmetic and copies ran while one was open for 13% of the time, Pallas kernels for 0%

profile of v2, /device:TPU:0, one launch (start us, length us, event | category | flops | bytes accessed | tf_op | source)
XLA Modules:
  0.0 292.7 jit_solution(1090381577667069957)
XLA Ops:
  3.1 5.1 %collective-permute-start.14 = (bf16[1536,128]{1,0:T(8,128)(2,1)S(1)}, bf16[1536,128]{1,0:T(8,128)(2,1)}, u32[]{:S(2)}, u32[]{:S(2)}) collective-permute-start(bf16[1536,128]{1,0:T(8,128)(2,1)S(1)} %bitcast.125), channel_id=1, source_target_pairs={{0,24},{1,16},{2,8},{3,0},{4,28},{5,20},{6,12},{7,4},{8,25},{9,17}... | collective-permute-start | bytes 1179656 | tf_op jit(solution)/shard_map/ppermute | solution.py:31
  10.9 6.4 %collective-permute-start.36 = (bf16[1536,128]{1,0:T(8,128)(2,1)S(1)}, bf16[1536,128]{1,0:T(8,128)(2,1)S(1)}, u32[]{:S(2)}, u32[]{:S(2)}) collective-permute-start(bf16[1536,128]{1,0:T(8,128)(2,1)S(1)} %bitcast.110), channel_id=1, source_target_pairs={{0,24},{1,16},{2,8},{3,0},{4,28},{5,20},{6,12},{7,4},{8,25},{9,17}... | collective-permute-start | bytes 1179656 | tf_op jit(solution)/shard_map/ppermute | solution.py:31
  18.3 9.9 %collective-permute-start.35 = (bf16[1536,128]{1,0:T(8,128)(2,1)S(1)}, bf16[1536,128]{1,0:T(8,128)(2,1)S(1)}, u32[]{:S(2)}, u32[]{:S(2)}) collective-permute-start(bf16[1536,128]{1,0:T(8,128)(2,1)S(1)} %bitcast.111), channel_id=1, source_target_pairs={{0,16},{1,24},{2,0},{3,8},{4,20},{5,28},{6,4},{7,12},{8,17},{9,25}... | collective-permute-start | bytes 1179656 | tf_op jit(solution)/shard_map/ppermute | solution.py:31
  28.2 5.4 %collective-permute-done.13 = bf16[1536,128]{1,0:T(8,128)(2,1)} collective-permute-done((bf16[1536,128]{1,0:T(8,128)(2,1)S(1)}, bf16[1536,128]{1,0:T(8,128)(2,1)}, u32[]{:S(2)}, u32[]{:S(2)}) %collective-permute-start.13) | collective-permute-done | bytes 393248 | tf_op jit(solution)/shard_map/ppermute | solution.py:31
  33.6 27.8 %collective-permute-start.34 = (bf16[1536,128]{1,0:T(8,128)(2,1)S(1)}, bf16[1536,128]{1,0:T(8,128)(2,1)S(1)}, u32[]{:S(2)}, u32[]{:S(2)}) collective-permute-start(bf16[1536,128]{1,0:T(8,128)(2,1)S(1)} %bitcast.112), channel_id=1, source_target_pairs={{0,8},{1,0},{2,24},{3,16},{4,12},{5,4},{6,28},{7,20},{8,9},{9,1},{... | collective-permute-start | bytes 1179656 | tf_op jit(solution)/shard_map/ppermute | solution.py:31
  62.2 5.0 %fusion.8 = f32[512,1536]{1,0:T(8,128)S(1)} fusion(bf16[1536,3072]{1,0:T(8,128)(2,1)} %param.4, s32[]{:T(128)S(6)} %select_n.61, bf16[1536,128]{1,0:T(8,128)(2,1)} %collective-permute-done.14, bf16[1536,128]{1,0:T(8,128)(2,1)} %collective-permute-done.13, bf16[1536,128]{1,0:T(8,128)(2,1)} %collective-permute-done.12, ...), kind=kOutput, calls=%fused_computation.12 | convolution fusion | flops 2422210560 | bytes 9437188 | tf_op jit(solution)/shard_map/dot_general | solution.py:84
  67.2 6.6 %collective-permute-start.24 = (bf16[1536,128]{1,0:T(8,128)(2,1)S(1)}, bf16[1536,128]{1,0:T(8,128)(2,1)S(1)}, u32[]{:S(2)}, u32[]{:S(2)}) collective-permute-start(bf16[1536,128]{1,0:T(8,128)(2,1)S(1)} %bitcast.121), channel_id=1, source_target_pairs={{0,16},{1,24},{2,0},{3,8},{4,20},{5,28},{6,4},{7,12},{8,17},{9,25}... | collective-permute-start | bytes 1179656 | tf_op jit(solution)/shard_map/ppermute | solution.py:31
  73.9 24.3 %collective-permute-start.23 = (bf16[1536,128]{1,0:T(8,128)(2,1)S(1)}, bf16[1536,128]{1,0:T(8,128)(2,1)S(1)}, u32[]{:S(2)}, u32[]{:S(2)}) collective-permute-start(bf16[1536,128]{1,0:T(8,128)(2,1)S(1)} %bitcast.122), channel_id=1, source_target_pairs={{0,8},{1,0},{2,24},{3,16},{4,12},{5,4},{6,28},{7,20},{8,9},{9,1},{... | collective-permute-start | bytes 1179656 | tf_op jit(solution)/shard_map/ppermute | solution.py:31
  99.0 2.7 fusion.4
  101.7 4.9 %collective-permute-start.2 = (bf16[1536,128]{1,0:T(8,128)(2,1)S(1)}, bf16[1536,128]{1,0:T(8,128)(2,1)S(1)}, u32[]{:S(2)}, u32[]{:S(2)}) collective-permute-start(bf16[1536,128]{1,0:T(8,128)(2,1)S(1)} %bitcast.116), channel_id=1, source_target_pairs={{0,16},{1,24},{2,0},{3,8},{4,20},{5,28},{6,4},{7,12},{8,17},{9,25}... | collective-permute-start | bytes 1179656 | tf_op jit(solution)/shard_map/ppermute | solution.py:31
  106.6 25.4 %collective-permute-start.1 = (bf16[1536,128]{1,0:T(8,128)(2,1)S(1)}, bf16[1536,128]{1,0:T(8,128)(2,1)S(1)}, u32[]{:S(2)}, u32[]{:S(2)}) collective-permute-start(bf16[1536,128]{1,0:T(8,128)(2,1)S(1)} %bitcast.117), channel_id=1, source_target_pairs={{0,8},{1,0},{2,24},{3,16},{4,12},{5,4},{6,28},{7,20},{8,9},{9,1},{... | collective-permute-start | bytes 1179656 | tf_op jit(solution)/shard_map/ppermute | solution.py:31
  132.9 4.3 %fusion.6 = f32[512,1536]{1,0:T(8,128)} fusion(bf16[1536,3072]{1,0:T(8,128)(2,1)S(1)} %bitcast.131, s32[]{:T(128)S(6)} %select_n.61, bf16[1536,128]{1,0:T(8,128)(2,1)S(1)} %collective-permute-done.25, bf16[1536,128]{1,0:T(8,128)(2,1)S(1)} %collective-permute-done.24, bf16[1536,128]{1,0:T(8,128)(2,1)S(1)} %collective-permute-done.23, ...), kind=kOutput, calls=%fused_computation.10 | convolution fusion | flops 2422210560 | bytes 9437188 | tf_op jit(solution)/shard_map/dot_general | solution.py:84
  137.8 2.7 collective-permute-done.1
  140.9 4.4 %fusion.10 = f32[512,1536]{1,0:T(8,128)} fusion(bf16[1536,3072]{1,0:T(8,128)(2,1)S(1)} %bitcast.131, s32[]{:T(128)S(6)} %select_n.61, bf16[1536,128]{1,0:T(8,128)(2,1)S(1)} %collective-permute-done.3, bf16[1536,128]{1,0:T(8,128)(2,1)S(1)} %collective-permute-done.2, bf16[1536,128]{1,0:T(8,128)(2,1)S(1)} %collective-permute-done.1, ...), kind=kOutput, calls=%fused_computation.14 | convolution fusion | flops 2422210560 | bytes 9437188 | tf_op jit(solution)/shard_map/dot_general | solution.py:84
  146.4 2.6 convolution_add_fusion.2
  150.1 4.6 %convolution_add_fusion.1 = f32[512,1536]{1,0:T(8,128)S(1)} fusion(f32[512,1536]{1,0:T(8,128)} %fusion.6, bf16[1536,3072]{1,0:T(8,128)(2,1)S(1)} %bitcast.131, s32[]{:T(128)S(6)} %select_n.63, bf16[1536,128]{1,0:T(8,128)(2,1)S(1)} %collective-permute-done.29, bf16[1536,128]{1,0:T(8,128)(2,1)S(1)} %collective-permute-done.28, ...), kind=kOutput, calls=%fused_computation.1 | convolution fusion | flops 2422996992 | bytes 12582916 | tf_op jit(solution)/shard_map/dot_general | solution.py:84
  155.6 14.9 %collective-permute-start.19 = (bf16[128,1536]{1,0:T(8,128)(2,1)S(1)}, bf16[128,1536]{1,0:T(8,128)(2,1)S(1)}, u32[]{:S(2)}, u32[]{:S(2)}) collective-permute-start(bf16[128,1536]{1,0:T(8,128)(2,1)S(1)} %get-tuple-element.5), channel_id=1, source_target_pairs={{0,1},{1,0},{2,3},{3,2},{4,5},{5,4},{6,7},{7,6},{8,9},{9,8},{10,11... | collective-permute-start | bytes 1179656 | tf_op jit(solution)/shard_map/ppermute | solution.py:31
  170.6 4.8 %convolution_add_fusion.3 = f32[512,1536]{1,0:T(8,128)S(1)} fusion(f32[512,1536]{1,0:T(8,128)} %fusion.10, bf16[1536,3072]{1,0:T(8,128)(2,1)S(1)} %bitcast.131, s32[]{:T(128)S(6)} %select_n.63, bf16[1536,128]{1,0:T(8,128)(2,1)S(1)} %collective-permute-done.7, bf16[1536,128]{1,0:T(8,128)(2,1)S(1)} %collective-permute-done.6, ...), kind=kOutput, calls=%fused_computation.3 | convolution fusion | flops 2422996992 | bytes 12582916 | tf_op jit(solution)/shard_map/dot_general | solution.py:84
  175.5 25.0 %collective-permute-start.21 = (bf16[128,1536]{1,0:T(8,128)(2,1)S(1)}, bf16[128,1536]{1,0:T(8,128)(2,1)S(1)}, u32[]{:S(2)}, u32[]{:S(2)}) collective-permute-start(bf16[128,1536]{1,0:T(8,128)(2,1)S(1)} %get-tuple-element.6), channel_id=1, source_target_pairs={{0,3},{1,2},{2,1},{3,0},{4,7},{5,6},{6,5},{7,4},{8,11},{9,10},{10,... | collective-permute-start | bytes 1179656 | tf_op jit(solution)/shard_map/ppermute | solution.py:31
  201.2 2.8 collective-permute-start.32
  204.0 2.6 convolution_add_fusion
  206.9 6.9 %collective-permute-done.21 = bf16[128,1536]{1,0:T(8,128)(2,1)S(1)} collective-permute-done((bf16[128,1536]{1,0:T(8,128)(2,1)S(1)}, bf16[128,1536]{1,0:T(8,128)(2,1)S(1)}, u32[]{:S(2)}, u32[]{:S(2)}) %collective-permute-start.21) | collective-permute-done | bytes 393248 | tf_op jit(solution)/shard_map/ppermute | solution.py:31
  213.9 7.0 %collective-permute-done.20 = bf16[128,1536]{1,0:T(8,128)(2,1)S(1)} collective-permute-done((bf16[128,1536]{1,0:T(8,128)(2,1)S(1)}, bf16[128,1536]{1,0:T(8,128)(2,1)S(1)}, u32[]{:S(2)}, u32[]{:S(2)}) %collective-permute-start.20) | collective-permute-done | bytes 393248 | tf_op jit(solution)/shard_map/ppermute | solution.py:31
  223.3 7.4 %collective-permute-done.32 = bf16[128,1536]{1,0:T(8,128)(2,1)S(1)} collective-permute-done((bf16[128,1536]{1,0:T(8,128)(2,1)S(1)}, bf16[128,1536]{1,0:T(8,128)(2,1)S(1)}, u32[]{:S(2)}, u32[]{:S(2)}) %collective-permute-start.32) | collective-permute-done | bytes 393248 | tf_op jit(solution)/shard_map/ppermute | solution.py:31
  230.8 7.0 %collective-permute-done.31 = bf16[128,1536]{1,0:T(8,128)(2,1)S(1)} collective-permute-done((bf16[128,1536]{1,0:T(8,128)(2,1)S(1)}, bf16[128,1536]{1,0:T(8,128)(2,1)S(1)}, u32[]{:S(2)}, u32[]{:S(2)}) %collective-permute-start.31) | collective-permute-done | bytes 393248 | tf_op jit(solution)/shard_map/ppermute | solution.py:31
  240.1 7.6 %collective-permute-done.10 = bf16[128,1536]{1,0:T(8,128)(2,1)S(1)} collective-permute-done((bf16[128,1536]{1,0:T(8,128)(2,1)S(1)}, bf16[128,1536]{1,0:T(8,128)(2,1)S(1)}, u32[]{:S(2)}, u32[]{:S(2)}) %collective-permute-start.10) | collective-permute-done | bytes 393248 | tf_op jit(solution)/shard_map/ppermute | solution.py:31
  247.7 7.0 %collective-permute-done.9 = bf16[128,1536]{1,0:T(8,128)(2,1)S(1)} collective-permute-done((bf16[128,1536]{1,0:T(8,128)(2,1)S(1)}, bf16[128,1536]{1,0:T(8,128)(2,1)S(1)}, u32[]{:S(2)}, u32[]{:S(2)}) %collective-permute-start.9) | collective-permute-done | bytes 393248 | tf_op jit(solution)/shard_map/ppermute | solution.py:31
  255.1 8.9 %collective-permute-done.43 = bf16[128,1536]{1,0:T(8,128)(2,1)S(1)} collective-permute-done((bf16[128,1536]{1,0:T(8,128)(2,1)S(1)}, bf16[128,1536]{1,0:T(8,128)(2,1)S(1)}, u32[]{:S(2)}, u32[]{:S(2)}) %collective-permute-start.43) | collective-permute-done | bytes 393248 | tf_op jit(solution)/shard_map/ppermute | solution.py:31
  264.0 6.3 %collective-permute-done.42 = bf16[128,1536]{1,0:T(8,128)(2,1)S(1)} collective-permute-done((bf16[128,1536]{1,0:T(8,128)(2,1)S(1)}, bf16[128,1536]{1,0:T(8,128)(2,1)S(1)}, u32[]{:S(2)}, u32[]{:S(2)}) %collective-permute-start.42) | collective-permute-done | bytes 393248 | tf_op jit(solution)/shard_map/ppermute | solution.py:31
  273.1 8.6 %collective-permute-start.46 = (bf16[3,128,128]{2,1,0:T(8,128)(2,1)S(1)}, bf16[3,128,128]{2,1,0:T(8,128)(2,1)S(1)}, u32[]{:S(2)}, u32[]{:S(2)}) collective-permute-start(bf16[3,128,128]{2,1,0:T(8,128)(2,1)S(1)} %reduce-precision_convert_fusion), channel_id=1, source_target_pairs={{0,16},{1,17},{2,18},{3,19},{4,20},{5,21},{6,22},{7,23},{8,24},{9,... | collective-permute-start | bytes 294920 | tf_op jit(solution)/shard_map/ppermute | solution.py:31
  285.2 2.7 collective-permute-start.49
  288.0 2.9 %collective-permute-done.46 = bf16[3,128,128]{2,1,0:T(8,128)(2,1)S(1)} collective-permute-done((bf16[3,128,128]{2,1,0:T(8,128)(2,1)S(1)}, bf16[3,128,128]{2,1,0:T(8,128)(2,1)S(1)}, u32[]{:S(2)}, u32[]{:S(2)}) %collective-permute-start.46) | collective-permute-done | bytes 98336 | tf_op jit(solution)/shard_map/ppermute | solution.py:31
  (112 shorter events, 26.9 us)
Async XLA Ops:
  8.2 25.4 %collective-permute-start.13 = (bf16[1536,128]{1,0:T(8,128)(2,1)S(1)}, bf16[1536,128]{1,0:T(8,128)(2,1)}, u32[]{:S(2)}, u32[]{:S(2)}) collective-permute-start(bf16[1536,128]{1,0:T(8,128)(2,1)S(1)} %bitcast.126), channel_id=1, source_target_pairs={{0,16},{1,24},{2,0},{3,8},{4,20},{5,28},{6,4},{7,12},{8,17},{9,25}... | collective-permute-start | bytes 1179656 | tf_op jit(solution)/shard_map/ppermute | solution.py:31
  9.7 51.7 %collective-permute-start.12 = (bf16[1536,128]{1,0:T(8,128)(2,1)S(1)}, bf16[1536,128]{1,0:T(8,128)(2,1)}, u32[]{:S(2)}, u32[]{:S(2)}) collective-permute-start(bf16[1536,128]{1,0:T(8,128)(2,1)S(1)} %bitcast.127), channel_id=1, source_target_pairs={{0,8},{1,0},{2,24},{3,16},{4,12},{5,4},{6,28},{7,20},{8,9},{9,1},{... | collective-permute-start | bytes 1179656 | tf_op jit(solution)/shard_map/ppermute | solution.py:31
  10.2 51.9 %collective-permute-start.11 = (bf16[1536,128]{1,0:T(8,128)(2,1)S(1)}, bf16[1536,128]{1,0:T(8,128)(2,1)S(1)}, u32[]{:S(2)}, u32[]{:S(2)}) collective-permute-start(bf16[1536,128]{1,0:T(8,128)(2,1)S(1)} %bitcast.128), channel_id=1, source_target_pairs={{0,0},{1,8},{2,16},{3,24},{4,4},{5,12},{6,20},{7,28},{8,1},{9,9},{... | collective-permute-start | bytes 1179656 | tf_op jit(solution)/shard_map/ppermute | solution.py:31
  10.9 56.4 %collective-permute-start.36 = (bf16[1536,128]{1,0:T(8,128)(2,1)S(1)}, bf16[1536,128]{1,0:T(8,128)(2,1)S(1)}, u32[]{:S(2)}, u32[]{:S(2)}) collective-permute-start(bf16[1536,128]{1,0:T(8,128)(2,1)S(1)} %bitcast.110), channel_id=1, source_target_pairs={{0,24},{1,16},{2,8},{3,0},{4,28},{5,20},{6,12},{7,4},{8,25},{9,17}... | collective-permute-start | bytes 1179656 | tf_op jit(solution)/shard_map/ppermute | solution.py:31
  18.3 55.6 %collective-permute-start.35 = (bf16[1536,128]{1,0:T(8,128)(2,1)S(1)}, bf16[1536,128]{1,0:T(8,128)(2,1)S(1)}, u32[]{:S(2)}, u32[]{:S(2)}) collective-permute-start(bf16[1536,128]{1,0:T(8,128)(2,1)S(1)} %bitcast.111), channel_id=1, source_target_pairs={{0,16},{1,24},{2,0},{3,8},{4,20},{5,28},{6,4},{7,12},{8,17},{9,25}... | collective-permute-start | bytes 1179656 | tf_op jit(solution)/shard_map/ppermute | solution.py:31
  33.6 64.6 %collective-permute-start.34 = (bf16[1536,128]{1,0:T(8,128)(2,1)S(1)}, bf16[1536,128]{1,0:T(8,128)(2,1)S(1)}, u32[]{:S(2)}, u32[]{:S(2)}) collective-permute-start(bf16[1536,128]{1,0:T(8,128)(2,1)S(1)} %bitcast.112), channel_id=1, source_target_pairs={{0,8},{1,0},{2,24},{3,16},{4,12},{5,4},{6,28},{7,20},{8,9},{9,1},{... | collective-permute-start | bytes 1179656 | tf_op jit(solution)/shard_map/ppermute | solution.py:31
  61.4 37.5 %collective-permute-start.33 = (bf16[1536,128]{1,0:T(8,128)(2,1)S(1)}, bf16[1536,128]{1,0:T(8,128)(2,1)S(1)}, u32[]{:S(2)}, u32[]{:S(2)}) collective-permute-start(bf16[1536,128]{1,0:T(8,128)(2,1)S(1)} %bitcast.113), channel_id=1, source_target_pairs={{0,0},{1,8},{2,16},{3,24},{4,4},{5,12},{6,20},{7,28},{8,1},{9,9},{... | collective-permute-start | bytes 1179656 | tf_op jit(solution)/shard_map/ppermute | solution.py:31
  62.1 39.5 %collective-permute-start.25 = (bf16[1536,128]{1,0:T(8,128)(2,1)S(1)}, bf16[1536,128]{1,0:T(8,128)(2,1)S(1)}, u32[]{:S(2)}, u32[]{:S(2)}) collective-permute-start(bf16[1536,128]{1,0:T(8,128)(2,1)S(1)} %bitcast.120), channel_id=1, source_target_pairs={{0,24},{1,16},{2,8},{3,0},{4,28},{5,20},{6,12},{7,4},{8,25},{9,17}... | collective-permute-start | bytes 1179656 | tf_op jit(solution)/shard_map/ppermute | solution.py:31
  67.2 39.4 %collective-permute-start.24 = (bf16[1536,128]{1,0:T(8,128)(2,1)S(1)}, bf16[1536,128]{1,0:T(8,128)(2,1)S(1)}, u32[]{:S(2)}, u32[]{:S(2)}) collective-permute-start(bf16[1536,128]{1,0:T(8,128)(2,1)S(1)} %bitcast.121), channel_id=1, source_target_pairs={{0,16},{1,24},{2,0},{3,8},{4,20},{5,28},{6,4},{7,12},{8,17},{9,25}... | collective-permute-start | bytes 1179656 | tf_op jit(solution)/shard_map/ppermute | solution.py:31
  73.9 58.1 %collective-permute-start.23 = (bf16[1536,128]{1,0:T(8,128)(2,1)S(1)}, bf16[1536,128]{1,0:T(8,128)(2,1)S(1)}, u32[]{:S(2)}, u32[]{:S(2)}) collective-permute-start(bf16[1536,128]{1,0:T(8,128)(2,1)S(1)} %bitcast.122), channel_id=1, source_target_pairs={{0,8},{1,0},{2,24},{3,16},{4,12},{5,4},{6,28},{7,20},{8,9},{9,1},{... | collective-permute-start | bytes 1179656 | tf_op jit(solution)/shard_map/ppermute | solution.py:31
  98.2 34.7 %collective-permute-start.22 = (bf16[1536,128]{1,0:T(8,128)(2,1)S(1)}, bf16[1536,128]{1,0:T(8,128)(2,1)S(1)}, u32[]{:S(2)}, u32[]{:S(2)}) collective-permute-start(bf16[1536,128]{1,0:T(8,128)(2,1)S(1)} %bitcast.123), channel_id=1, source_target_pairs={{0,0},{1,8},{2,16},{3,24},{4,4},{5,12},{6,20},{7,28},{8,1},{9,9},{... | collective-permute-start | bytes 1179656 | tf_op jit(solution)/shard_map/ppermute | solution.py:31
  98.9 38.4 %collective-permute-start.3 = (bf16[1536,128]{1,0:T(8,128)(2,1)S(1)}, bf16[1536,128]{1,0:T(8,128)(2,1)S(1)}, u32[]{:S(2)}, u32[]{:S(2)}) collective-permute-start(bf16[1536,128]{1,0:T(8,128)(2,1)S(1)} %bitcast.115), channel_id=1, source_target_pairs={{0,24},{1,16},{2,8},{3,0},{4,28},{5,20},{6,12},{7,4},{8,25},{9,17}... | collective-permute-start | bytes 1179656 | tf_op jit(solution)/shard_map/ppermute | solution.py:31
  101.7 36.0 %collective-permute-start.2 = (bf16[1536,128]{1,0:T(8,128)(2,1)S(1)}, bf16[1536,128]{1,0:T(8,128)(2,1)S(1)}, u32[]{:S(2)}, u32[]{:S(2)}) collective-permute-start(bf16[1536,128]{1,0:T(8,128)(2,1)S(1)} %bitcast.116), channel_id=1, source_target_pairs={{0,16},{1,24},{2,0},{3,8},{4,20},{5,28},{6,4},{7,12},{8,17},{9,25}... | collective-permute-start | bytes 1179656 | tf_op jit(solution)/shard_map/ppermute | solution.py:31
  106.6 33.8 %collective-permute-start.1 = (bf16[1536,128]{1,0:T(8,128)(2,1)S(1)}, bf16[1536,128]{1,0:T(8,128)(2,1)S(1)}, u32[]{:S(2)}, u32[]{:S(2)}) collective-permute-start(bf16[1536,128]{1,0:T(8,128)(2,1)S(1)} %bitcast.117), channel_id=1, source_target_pairs={{0,8},{1,0},{2,24},{3,16},{4,12},{5,4},{6,28},{7,20},{8,9},{9,1},{... | collective-permute-start | bytes 1179656 | tf_op jit(solution)/shard_map/ppermute | solution.py:31
  132.8 42.7 %collective-permute-start.40 = (bf16[1536,128]{1,0:T(8,128)(2,1)S(1)}, bf16[1536,128]{1,0:T(8,128)(2,1)S(1)}, u32[]{:S(2)}, u32[]{:S(2)}) collective-permute-start(bf16[1536,128]{1,0:T(8,128)(2,1)S(1)} %collective-permute-done.36), channel_id=1, source_target_pairs={{0,4},{1,5},{2,6},{3,7},{4,0},{5,1},{6,2},{7,3},{8,12},{9,13},{10,... | collective-permute-start | bytes 1179656 | tf_op jit(solution)/shard_map/ppermute | solution.py:31
  154.8 45.6 %collective-permute-start.39 = (bf16[1536,128]{1,0:T(8,128)(2,1)S(1)}, bf16[1536,128]{1,0:T(8,128)(2,1)S(1)}, u32[]{:S(2)}, u32[]{:S(2)}) collective-permute-start(bf16[1536,128]{1,0:T(8,128)(2,1)S(1)} %collective-permute-done.35), channel_id=1, source_target_pairs={{0,4},{1,5},{2,6},{3,7},{4,0},{5,1},{6,2},{7,3},{8,12},{9,13},{10,... | collective-permute-start | bytes 1179656 | tf_op jit(solution)/shard_map/ppermute | solution.py:31
  155.1 45.4 %collective-permute-start.38 = (bf16[1536,128]{1,0:T(8,128)(2,1)S(1)}, bf16[1536,128]{1,0:T(8,128)(2,1)S(1)}, u32[]{:S(2)}, u32[]{:S(2)}) collective-permute-start(bf16[1536,128]{1,0:T(8,128)(2,1)S(1)} %collective-permute-done.34), channel_id=1, source_target_pairs={{0,4},{1,5},{2,6},{3,7},{4,0},{5,1},{6,2},{7,3},{8,12},{9,13},{10,... | collective-permute-start | bytes 1179656 | tf_op jit(solution)/shard_map/ppermute | solution.py:31
  155.4 45.7 %collective-permute-start.37 = (bf16[1536,128]{1,0:T(8,128)(2,1)S(1)}, bf16[1536,128]{1,0:T(8,128)(2,1)S(1)}, u32[]{:S(2)}, u32[]{:S(2)}) collective-permute-start(bf16[1536,128]{1,0:T(8,128)(2,1)S(1)} %collective-permute-done.33), channel_id=1, source_target_pairs={{0,4},{1,5},{2,6},{3,7},{4,0},{5,1},{6,2},{7,3},{8,12},{9,13},{10,... | collective-permute-start | bytes 1179656 | tf_op jit(solution)/shard_map/ppermute | solution.py:31
  155.6 51.2 %collective-permute-start.19 = (bf16[128,1536]{1,0:T(8,128)(2,1)S(1)}, bf16[128,1536]{1,0:T(8,128)(2,1)S(1)}, u32[]{:S(2)}, u32[]{:S(2)}) collective-permute-start(bf16[128,1536]{1,0:T(8,128)(2,1)S(1)} %get-tuple-element.5), channel_id=1, source_target_pairs={{0,1},{1,0},{2,3},{3,2},{4,5},{5,4},{6,7},{7,6},{8,9},{9,8},{10,11... | collective-permute-start | bytes 1179656 | tf_op jit(solution)/shard_map/ppermute | solution.py:31
  175.5 38.3 %collective-permute-start.21 = (bf16[128,1536]{1,0:T(8,128)(2,1)S(1)}, bf16[128,1536]{1,0:T(8,128)(2,1)S(1)}, u32[]{:S(2)}, u32[]{:S(2)}) collective-permute-start(bf16[128,1536]{1,0:T(8,128)(2,1)S(1)} %get-tuple-element.6), channel_id=1, source_target_pairs={{0,3},{1,2},{2,1},{3,0},{4,7},{5,6},{6,5},{7,4},{8,11},{9,10},{10,... | collective-permute-start | bytes 1179656 | tf_op jit(solution)/shard_map/ppermute | solution.py:31
  200.5 20.4 %collective-permute-start.20 = (bf16[128,1536]{1,0:T(8,128)(2,1)S(1)}, bf16[128,1536]{1,0:T(8,128)(2,1)S(1)}, u32[]{:S(2)}, u32[]{:S(2)}) collective-permute-start(bf16[128,1536]{1,0:T(8,128)(2,1)S(1)} %get-tuple-element.7), channel_id=1, source_target_pairs={{0,2},{1,3},{2,0},{3,1},{4,6},{5,7},{6,4},{7,5},{8,10},{9,11},{10,... | collective-permute-start | bytes 1179656 | tf_op jit(solution)/shard_map/ppermute | solution.py:31
  200.5 21.4 %collective-permute-start.30 = (bf16[128,1536]{1,0:T(8,128)(2,1)S(1)}, bf16[128,1536]{1,0:T(8,128)(2,1)S(1)}, u32[]{:S(2)}, u32[]{:S(2)}) collective-permute-start(bf16[128,1536]{1,0:T(8,128)(2,1)S(1)} %get-tuple-element.8), channel_id=1, source_target_pairs={{0,1},{1,0},{2,3},{3,2},{4,5},{5,4},{6,7},{7,6},{8,9},{9,8},{10,11... | collective-permute-start | bytes 1179656 | tf_op jit(solution)/shard_map/ppermute | solution.py:31
  201.2 29.6 %collective-permute-start.32 = (bf16[128,1536]{1,0:T(8,128)(2,1)S(1)}, bf16[128,1536]{1,0:T(8,128)(2,1)S(1)}, u32[]{:S(2)}, u32[]{:S(2)}) collective-permute-start(bf16[128,1536]{1,0:T(8,128)(2,1)S(1)} %get-tuple-element.9), channel_id=1, source_target_pairs={{0,3},{1,2},{2,1},{3,0},{4,7},{5,6},{6,5},{7,4},{8,11},{9,10},{10,... | collective-permute-start | bytes 1179656 | tf_op jit(solution)/shard_map/ppermute | solution.py:31
  206.8 31.0 %collective-permute-start.31 = (bf16[128,1536]{1,0:T(8,128)(2,1)S(1)}, bf16[128,1536]{1,0:T(8,128)(2,1)S(1)}, u32[]{:S(2)}, u32[]{:S(2)}) collective-permute-start(bf16[128,1536]{1,0:T(8,128)(2,1)S(1)} %get-tuple-element.10), channel_id=1, source_target_pairs={{0,2},{1,3},{2,0},{3,1},{4,6},{5,7},{6,4},{7,5},{8,10},{9,11},{10,... | collective-permute-start | bytes 1179656 | tf_op jit(solution)/shard_map/ppermute | solution.py:31
  213.9 24.8 %collective-permute-start.8 = (bf16[128,1536]{1,0:T(8,128)(2,1)S(1)}, bf16[128,1536]{1,0:T(8,128)(2,1)S(1)}, u32[]{:S(2)}, u32[]{:S(2)}) collective-permute-start(bf16[128,1536]{1,0:T(8,128)(2,1)S(1)} %get-tuple-element.2), channel_id=1, source_target_pairs={{0,1},{1,0},{2,3},{3,2},{4,5},{5,4},{6,7},{7,6},{8,9},{9,8},{10,11... | collective-permute-start | bytes 1179656 | tf_op jit(solution)/shard_map/ppermute | solution.py:31
  220.9 26.8 %collective-permute-start.10 = (bf16[128,1536]{1,0:T(8,128)(2,1)S(1)}, bf16[128,1536]{1,0:T(8,128)(2,1)S(1)}, u32[]{:S(2)}, u32[]{:S(2)}) collective-permute-start(bf16[128,1536]{1,0:T(8,128)(2,1)S(1)} %get-tuple-element.3), channel_id=1, source_target_pairs={{0,3},{1,2},{2,1},{3,0},{4,7},{5,6},{6,5},{7,4},{8,11},{9,10},{10,... | collective-permute-start | bytes 1179656 | tf_op jit(solution)/shard_map/ppermute | solution.py:31
  221.9 32.7 %collective-permute-start.9 = (bf16[128,1536]{1,0:T(8,128)(2,1)S(1)}, bf16[128,1536]{1,0:T(8,128)(2,1)S(1)}, u32[]{:S(2)}, u32[]{:S(2)}) collective-permute-start(bf16[128,1536]{1,0:T(8,128)(2,1)S(1)} %get-tuple-element.4), channel_id=1, source_target_pairs={{0,2},{1,3},{2,0},{3,1},{4,6},{5,7},{6,4},{7,5},{8,10},{9,11},{10,... | collective-permute-start | bytes 1179656 | tf_op jit(solution)/shard_map/ppermute | solution.py:31
  230.8 24.3 %collective-permute-start.41 = (bf16[128,1536]{1,0:T(8,128)(2,1)S(1)}, bf16[128,1536]{1,0:T(8,128)(2,1)S(1)}, u32[]{:S(2)}, u32[]{:S(2)}) collective-permute-start(bf16[128,1536]{1,0:T(8,128)(2,1)S(1)} %get-tuple-element.11), channel_id=1, source_target_pairs={{0,1},{1,0},{2,3},{3,2},{4,5},{5,4},{6,7},{7,6},{8,9},{9,8},{10,11... | collective-permute-start | bytes 1179656 | tf_op jit(solution)/shard_map/ppermute | solution.py:31
  237.8 26.2 %collective-permute-start.43 = (bf16[128,1536]{1,0:T(8,128)(2,1)S(1)}, bf16[128,1536]{1,0:T(8,128)(2,1)S(1)}, u32[]{:S(2)}, u32[]{:S(2)}) collective-permute-start(bf16[128,1536]{1,0:T(8,128)(2,1)S(1)} %get-tuple-element.12), channel_id=1, source_target_pairs={{0,3},{1,2},{2,1},{3,0},{4,7},{5,6},{6,5},{7,4},{8,11},{9,10},{10,... | collective-permute-start | bytes 1179656 | tf_op jit(solution)/shard_map/ppermute | solution.py:31
  238.7 31.6 %collective-permute-start.42 = (bf16[128,1536]{1,0:T(8,128)(2,1)S(1)}, bf16[128,1536]{1,0:T(8,128)(2,1)S(1)}, u32[]{:S(2)}, u32[]{:S(2)}) collective-permute-start(bf16[128,1536]{1,0:T(8,128)(2,1)S(1)} %get-tuple-element.13), channel_id=1, source_target_pairs={{0,2},{1,3},{2,0},{3,1},{4,6},{5,7},{6,4},{7,5},{8,10},{9,11},{10,... | collective-permute-start | bytes 1179656 | tf_op jit(solution)/shard_map/ppermute | solution.py:31
  255.0 17.9 %collective-permute-start.44 = (bf16[3,128,128]{2,1,0:T(8,128)(2,1)S(1)}, bf16[3,128,128]{2,1,0:T(8,128)(2,1)S(1)}, u32[]{:S(2)}, u32[]{:S(2)}) collective-permute-start(bf16[3,128,128]{2,1,0:T(8,128)(2,1)S(1)} %fusion.94), channel_id=1, source_target_pairs={{0,4},{1,5},{2,6},{3,7},{4,0},{5,1},{6,2},{7,3},{8,12},{9,13},{10,... | collective-permute-start | bytes 294920 | tf_op jit(solution)/shard_map/ppermute | solution.py:31
  273.1 17.8 %collective-permute-start.46 = (bf16[3,128,128]{2,1,0:T(8,128)(2,1)S(1)}, bf16[3,128,128]{2,1,0:T(8,128)(2,1)S(1)}, u32[]{:S(2)}, u32[]{:S(2)}) collective-permute-start(bf16[3,128,128]{2,1,0:T(8,128)(2,1)S(1)} %reduce-precision_convert_fusion), channel_id=1, source_target_pairs={{0,16},{1,17},{2,18},{3,19},{4,20},{5,21},{6,22},{7,23},{8,24},{9,... | collective-permute-start | bytes 294920 | tf_op jit(solution)/shard_map/ppermute | solution.py:31
  (24 other events, 318.9 us)
